TPU v7x, 256 devices: a 8x8x2 block of a 8x8x16 slice. The times are simulated.
256 devices in a mesh: groups: 2 (over z), rows: 16 (over y, core), cols: 8 (over x).
Axes of the slice: x: 8, y: 8, z: 2, core: 2. Of those that a mesh axis runs over, the one named last changes fastest.
The devices are a block of a 8x8x16 slice.
Arguments:
- pair_state: float32 [768, 384, 128], P(('groups', 'rows'), 'cols'), parts along dimension 0, may hold values from -6 to 6
- token_mask: int32 [768], P('groups'), parts along dimension 0, may hold values 0 or 1
- norm_gain: float32 [2, 128], replicated, may hold values from 0.25 to 1.75
- norm_bias: float32 [2, 128], replicated, may hold values from -3 to 3
- proj_weight: float32 [2, 128, 512], replicated, may hold values from -0.5 to 0.5
- gate_weight: float32 [2, 128, 128], replicated, may hold values from -0.5 to 0.5
- out_gain: float32 [2, 128], replicated, may hold values from 0.25 to 1.75
- out_bias: float32 [2, 128], replicated, may hold values from -3 to 3
- out_weight: float32 [2, 128, 128], replicated, may hold values from -0.5 to 0.5
Outputs:
- pair_out: float32 [768, 384, 128], P(('groups', 'rows'), 'cols'), parts along dimension 0
There are 2 independent parts, one for each index of `groups`. A program takes and returns all parts, laid end to end along the dimension named above; an argument that names none is the same for every part. Nothing has to cross between parts.
All inputs are finite; a program needn't handle non-finite values.
Results may differ from a plain program's by a relative error of at most 0.0001.
Values sent between devices are 32-bit elements; how exact they have to be, the bound alone decides.
A program may use at most 128 MiB of HBM per device.

v0:
```python
import jax
import jax.numpy as jnp
from jax import lax
from jax.sharding import PartitionSpec as P

eps = 1e-05


def normalize(values, gain, shift):
    center = values - jnp.mean(values, axis=-1, keepdims=True)
    spread = jnp.mean(center * center, axis=-1, keepdims=True)
    return center * lax.rsqrt(spread + eps) * gain + shift


def project(state, pair_mask, segment, norm_gain, norm_bias, proj_weight, gate_weight):
    width = proj_weight.shape[2] // 4
    normed = normalize(state, norm_gain[segment], norm_bias[segment])
    hidden = jnp.einsum(
        "ijc,cf->ijf", normed, proj_weight[segment], precision=lax.Precision.HIGHEST
    )
    left_side = (
        pair_mask[:, :, None]
        * jax.nn.sigmoid(hidden[:, :, :width])
        * hidden[:, :, width : 2 * width]
    )
    right_side = (
        pair_mask[:, :, None]
        * jax.nn.sigmoid(hidden[:, :, 2 * width : 3 * width])
        * hidden[:, :, 3 * width :]
    )
    gating = jax.nn.sigmoid(
        jnp.einsum("ijc,cd->ijd", normed, gate_weight[segment], precision=lax.Precision.HIGHEST)
    )
    return (left_side, right_side, gating)


def finish(state, mixed, gating, segment, out_gain, out_bias, out_weight):
    result = jnp.einsum(
        "ijh,hc->ijc",
        normalize(mixed, out_gain[segment], out_bias[segment]),
        out_weight[segment],
        precision=lax.Precision.HIGHEST,
    )
    return state + gating * result


def body(
    pair_state,
    token_mask,
    norm_gain,
    norm_bias,
    proj_weight,
    gate_weight,
    out_gain,
    out_bias,
    out_weight,
):
    row_count = pair_state.shape[0]
    col_count = pair_state.shape[1]
    row_start = lax.axis_index("rows") * row_count
    col_start = lax.axis_index("cols") * col_count
    maskf = token_mask.astype(jnp.float32)
    row_mask = lax.dynamic_slice_in_dim(maskf, row_start, row_count)
    col_mask = lax.dynamic_slice_in_dim(maskf, col_start, col_count)
    pair_mask = row_mask[:, None] * col_mask[None, :]
    left_side, right_side, gating = project(
        pair_state, pair_mask, 0, norm_gain, norm_bias, proj_weight, gate_weight
    )
    partial_out = jnp.einsum(
        "ikh,jkh->ijh",
        left_side,
        lax.all_gather(right_side, "rows", axis=0, tiled=True),
        precision=lax.Precision.HIGHEST,
    )
    mixed = lax.psum_scatter(partial_out, "cols", scatter_dimension=1, tiled=True)
    updated = finish(pair_state, mixed, gating, 0, out_gain, out_bias, out_weight)
    left_next, right_next, gate_next = project(
        updated, pair_mask, 1, norm_gain, norm_bias, proj_weight, gate_weight
    )
    partial_in = jnp.einsum(
        "kih,kjh->ijh",
        lax.all_gather(left_next, "cols", axis=1, tiled=True),
        right_next,
        precision=lax.Precision.HIGHEST,
    )
    mixed_next = lax.psum_scatter(partial_in, "rows", scatter_dimension=0, tiled=True)
    return finish(updated, mixed_next, gate_next, 1, out_gain, out_bias, out_weight)


def solution(mesh):
    placed = (P(("groups", "rows"), "cols", None), P("groups"), P(), P(), P(), P(), P(), P(), P())
    return jax.shard_map(
        body,
        mesh=mesh,
        in_specs=placed,
        out_specs=P(("groups", "rows"), "cols", None),
        check_vma=False,
    )
```

profile of v0, /device:TPU:514, one launch (start us, length us, event | category | flops | bytes accessed | tf_op | source)
XLA Modules:
  0.0 397.2 jit_solution(2512777455134591097)
XLA Ops:
  6.6 0.7 convert_element_type.3
  7.2 0.1 dynamic_slice.6
  7.3 0.1 dynamic_slice.7
  7.4 1.3 reduce_sum.72
  8.7 1.5 multiply_reduce_fusion.3
  10.2 0.1 broadcast_multiply_fusion
  10.3 0.8 slice_bitcast_fusion.2
  11.0 3.2 fusion.29
  14.2 1.2 slice_multiply_fusion.2
  15.4 0.1 all-gather.3.cloned.1.call-update
  15.4 0.1 reduce-scatter.3.cloned.1.call-start
  15.5 0.5 copy.47
  16.1 79.5 %all-gather.3.cloned.1.call-done = f32[384,48,128]{2,1,0:T(8,128)} async-done(((f32[24,48,128]{2,1,0:T(8,128)}), f32[384,48,128]{2,1,0:T(8,128)}) %all-gather.3.cloned.1.call-update) | async-done | bytes 9437200 | tf_op jit(solution)/shard_map/all_gather | solution.py:72
  95.6 21.7 %copy.46 = f32[384,48,128]{1,0,2:T(8,128)} copy(f32[384,48,128]{2,1,0:T(8,128)} %all-gather.3.cloned.1.call-done) | data formatting | bytes 18874368 | tf_op jit(solution)/shard_map/all_gather | solution.py:72
  117.3 31.6 %convolution_bitcast_fusion.1 = f32[24,384,128]{1,0,2:T(8,128)} fusion(f32[384,48,128]{1,0,2:T(8,128)} %copy.46, f32[24,48,128]{1,0,2:T(8,128)S(1)} %copy.47), kind=kOutput, calls=%fused_computation.1 | convolution fusion | flops 679477248 | bytes 14745600 | tf_op jit(solution)/shard_map/ikh,jkh->ijh/dot_general | solution.py:69
  148.9 6.0 %copy.48 = f32[24,384,128]{2,0,1:T(8,128)} copy(f32[24,384,128]{1,0,2:T(8,128)} %convolution_bitcast_fusion.1) | data formatting | bytes 9437184 | tf_op jit(solution)/shard_map/ikh,jkh->ijh/transpose | solution.py:69
  154.9 0.1 reduce-scatter.3.cloned.1.call-update
  155.0 0.2 all-gather.5.cloned.1.call-start
  155.2 0.3 copy-done.3
  155.6 0.0 copy-done.4
  155.6 0.4 copy-done
  156.0 0.0 copy-done.5
  156.0 0.8 fusion.7
  156.8 56.9 %reduce-scatter.3.cloned.1.call-done = f32[24,48,128]{2,0,1:T(8,128)} async-done(((f32[24,384,128]{2,0,1:T(8,128)}), f32[24,48,128]{2,0,1:T(8,128)}) %reduce-scatter.3.cloned.1.call-update) | async-done | bytes 589840 | tf_op jit(solution)/shard_map/reduce_scatter | solution.py:75
  213.7 1.3 reduce_sum.74
  215.0 0.1 copy.49
  215.1 0.1 copy.50
  215.2 1.5 multiply_reduce_fusion.2
  216.6 0.1 copy.51
  216.7 0.1 copy.52
  216.8 1.4 multiply_add_fusion.1
  218.3 0.7 fusion.63
  219.0 0.4 multiply_reduce_fusion.1
  219.4 2.1 fusion.30
  221.5 1.2 slice_multiply_fusion
  222.6 0.1 all-gather.5.cloned.1.call-update
  222.7 0.1 reduce-scatter.5.cloned.1.call-start
  222.8 0.5 copy.54
  223.3 59.2 %all-gather.5.cloned.1.call-done = f32[24,384,128]{2,1,0:T(8,128)} async-done(((f32[24,48,128]{2,1,0:T(8,128)}), f32[24,384,128]{2,1,0:T(8,128)}) %all-gather.5.cloned.1.call-update) | async-done | bytes 4718608 | tf_op jit(solution)/shard_map/all_gather | solution.py:82
  282.6 6.2 %copy.55 = f32[24,384,128]{1,0,2:T(8,128)} copy(f32[24,384,128]{2,1,0:T(8,128)} %all-gather.5.cloned.1.call-done) | data formatting | bytes 9437184 | tf_op jit(solution)/shard_map/all_gather | solution.py:82
  288.8 11.8 %convolution_bitcast_fusion = f32[384,48,128]{0,1,2:T(8,128)} fusion(f32[24,48,128]{1,0,2:T(8,128)S(1)} %copy.54, f32[24,384,128]{1,0,2:T(8,128)} %copy.55), kind=kOutput, calls=%fused_computation | convolution fusion | flops 679477248 | bytes 14745600 | tf_op jit(solution)/shard_map/kih,kjh->ijh/dot_general | solution.py:80
  300.5 9.8 %copy.56 = f32[384,48,128]{2,1,0:T(8,128)} copy(f32[384,48,128]{0,1,2:T(8,128)} %convolution_bitcast_fusion) | data formatting | bytes 18874368 | tf_op jit(solution)/shard_map/kih,kjh->ijh/transpose | solution.py:80
  310.3 0.1 reduce-scatter.5.cloned.1.call-update
  310.4 0.8 fusion.3
  311.2 74.0 %reduce-scatter.5.cloned.1.call-done = f32[24,48,128]{2,1,0:T(8,128)} async-done(((f32[384,48,128]{2,1,0:T(8,128)}), f32[24,48,128]{2,1,0:T(8,128)}) %reduce-scatter.5.cloned.1.call-update) | async-done | bytes 589840 | tf_op jit(solution)/shard_map/reduce_scatter | solution.py:86
  385.2 1.3 reduce_sum.78
  386.5 1.5 multiply_reduce_fusion
  388.0 2.7 fusion
  (18 shorter events, 0.1 us)
Async XLA Ops:
  6.5 89.1 %all-gather.3.cloned.1.call-start = ((), (), s32[]{:S(2)}) async-start(), calls=%async_computation.2 | async-start | bytes 10027008 | tf_op jit(solution)/shard_map/all_gather | solution.py:72
  15.4 198.3 %reduce-scatter.3.cloned.1.call-start = ((), (), s32[]{:S(2)}) async-start(), calls=%async_computation.3 | async-start | bytes 5308416 | tf_op jit(solution)/shard_map/reduce_scatter | solution.py:75
  154.9 0.7 copy-start.3
  154.9 0.7 copy-start.4
  154.9 1.1 copy-start
  154.9 1.1 copy-start.5
  154.9 63.3 %copy-start.2 = (f32[2,128,128]{2,1,0:T(8,128)S(1)}, f32[2,128,128]{2,1,0:T(8,128)}, u32[]{:S(2)}) copy-start(f32[2,128,128]{2,1,0:T(8,128)} %param.17) | copy-start | bytes 393220
  155.0 64.4 %copy-start.1 = (f32[2,128,512]{2,1,0:T(8,128)S(1)}, f32[2,128,512]{2,1,0:T(8,128)}, u32[]{:S(2)}) copy-start(f32[2,128,512]{2,1,0:T(8,128)} %param.13) | copy-start | bytes 1572868
  155.0 127.6 %all-gather.5.cloned.1.call-start = ((), (), s32[]{:S(2)}) async-start(), calls=%async_computation.4 | async-start | bytes 5308416 | tf_op jit(solution)/shard_map/all_gather | solution.py:82
  222.7 162.5 %reduce-scatter.5.cloned.1.call-start = ((), (), s32[]{:S(2)}) async-start(), calls=%async_computation.5 | async-start | bytes 10027008 | tf_op jit(solution)/shard_map/reduce_scatter | solution.py:86
Sparse Core Ops, SparseCore 0:
  15.6 79.9 all-gather.2
  155.1 58.5 reduce-scatter.2
  222.8 59.6 all-gather.4
  310.5 74.6 reduce-scatter.4
where the time goes:
time: 398 us; the launch traced here: 397 us
  waiting for transfers between devices  270 us (68%)
  matrix products  53.6 us (13%)
  local copies, waits for them, and re-layouts  46.8 us (12%)
  other arithmetic  13.3 us (3%)
  between operations  13.3 us (3%)
    all_gather x1, waiting for transfers between devices, body(): lax.all_gather(right_side, 'rows', axis=0, tiled=True)  79.5 us
    reduce_scatter x1, waiting for transfers between devices, body(): lax.psum_scatter(partial_in, 'rows', scatter_dimension=0, tiled=True)  74 us
    all_gather x1, waiting for transfers between devices, body(): lax.all_gather(left_next, 'cols', axis=1, tiled=True)  59.2 us
    reduce_scatter x1, waiting for transfers between devices, body(): lax.psum_scatter(partial_out, 'cols', scatter_dimension=1, tiled=True)  56.9 us
    dot_general x1, matrix products, body(): jnp.einsum('ikh,jkh->ijh', left_side, lax.all_gather(right_side, 'rows',...  31.6 us
    all_gather x1, local copies, waits for them, and re-layouts, body(): lax.all_gather(right_side, 'rows', axis=0, tiled=True)  21.7 us
    dot_general x1, matrix products, body(): jnp.einsum('kih,kjh->ijh', lax.all_gather(left_next, 'cols', axis=1, tile...  11.8 us
    transpose x1, local copies, waits for them, and re-layouts, body(): jnp.einsum('kih,kjh->ijh', lax.all_gather(left_next, 'cols', axis=1, tile...  9.8 us
  transfers between devices with their start and end apart: 4, of which 4 were waited for; matrix products, arithmetic and copies ran while one was open for 1% of the time, Pallas kernels for 0%

commit v1 on v0

--- a/solution.py
+++ b/solution.py
@@ -69,7 +69,9 @@
     partial_out = jnp.einsum(
         "ikh,jkh->ijh",
         left_side,
-        lax.all_gather(right_side, "rows", axis=0, tiled=True),
+        jnp.concatenate(
+            lax.all_to_all(jnp.stack([right_side] * lax.axis_size("rows")), "rows", 0, 0), axis=0
+        ),
         precision=lax.Precision.HIGHEST,
     )
     mixed = lax.psum_scatter(partial_out, "cols", scatter_dimension=1, tiled=True)

time: 398 us -> 519 us (1.30)
  waiting for transfers between devices: 270 us -> 407 us
  matrix products: 53.6 us -> 31.9 us
  starting transfers between devices: 0.38 us -> 14.1 us
  local copies, waits for them, and re-layouts: 46.8 us -> 39.5 us
    all_to_all x0 -> x1, waiting for transfers between devices: none -> 206 us  [body(): lax.all_to_all(jnp.stack([right_side] * lax.axis_size('rows')), 'rows', 0...]
    all_gather x1 -> x0, waiting for transfers between devices: 79.5 us -> none  [body(): lax.all_gather(right_side, 'rows', axis=0, tiled=True)]
    dot_general x1, matrix products: 31.6 us -> 9.88 us  [body(): jnp.einsum('ikh,jkh->ijh', left_side, jnp.concatenate(lax.all_to_all(jnp....]
    all_gather x1 -> x0, local copies, waits for them, and re-layouts: 21.7 us -> none  [body(): lax.all_gather(right_side, 'rows', axis=0, tiled=True)]
    all_to_all x0 -> x1, starting transfers between devices: none -> 13.5 us  [body(): lax.all_to_all(jnp.stack([right_side] * lax.axis_size('rows')), 'rows', 0...]
    reduce_scatter x1, waiting for transfers between devices: 56.9 us -> 67.5 us  [body(): lax.psum_scatter(partial_out, 'cols', scatter_dimension=1, tiled=True)]
    reshape x0 -> x1, local copies, waits for them, and re-layouts: none -> 9.76 us  [body(): jnp.concatenate(lax.all_to_all(jnp.stack([right_side] * lax.axis_size('ro...]
where the time goes in v1:
time: 519 us; the launch traced here: 518 us
  waiting for transfers between devices  407 us (78%)
  local copies, waits for them, and re-layouts  39.5 us (8%)
  matrix products  31.9 us (6%)
  starting transfers between devices  14.1 us (3%)
  between operations  13.3 us (3%)
  other arithmetic  12.5 us (2%)
    all_to_all x1, waiting for transfers between devices, body(): lax.all_to_all(jnp.stack([right_side] * lax.axis_size('rows')), 'rows', 0...  206 us
    reduce_scatter x1, waiting for transfers between devices, body(): lax.psum_scatter(partial_in, 'rows', scatter_dimension=0, tiled=True)  73.9 us
    reduce_scatter x1, waiting for transfers between devices, body(): lax.psum_scatter(partial_out, 'cols', scatter_dimension=1, tiled=True)  67.5 us
    all_gather x1, waiting for transfers between devices, body(): lax.all_gather(left_next, 'cols', axis=1, tiled=True)  59 us
    all_to_all x1, starting transfers between devices, body(): lax.all_to_all(jnp.stack([right_side] * lax.axis_size('rows')), 'rows', 0...  13.5 us
    dot_general x1, matrix products, body(): jnp.einsum('kih,kjh->ijh', lax.all_gather(left_next, 'cols', axis=1, tile...  11.8 us
  transfers between devices with their start and end apart: 4, of which 4 were waited for; matrix products, arithmetic and copies ran while one was open for 1% of the time, Pallas kernels for 0%

profile of v1, /device:TPU:514, one launch (start us, length us, event | category | flops | bytes accessed | tf_op | source)
XLA Modules:
  0.0 517.8 jit_solution(15215196038824469978)
XLA Ops:
  6.5 0.7 convert_element_type.3
  7.2 0.1 dynamic_slice.6
  7.3 0.1 dynamic_slice.7
  7.4 1.3 reduce_sum.72
  8.7 1.5 multiply_reduce_fusion.3
  10.2 0.1 broadcast_multiply_fusion
  10.3 0.8 slice_bitcast_fusion.2
  11.0 3.2 fusion.29
  14.2 0.3 slice_multiply_fusion.2
  14.6 4.6 stack.2
  19.1 13.5 %all-to-all-start = ((f32[16,24,48,128]{3,2,1,0:T(8,128)}), f32[16,24,48,128]{3,2,1,0:T(8,128)}, u32[]{:S(2)}, u32[]{:S(2)}) async-start(f32[16,24,48,128]{3,2,1,0:T(8,128)} %stack.2), calls=%async_computation | async-start | bytes 18874368 | tf_op jit(solution)/shard_map/all_to_all | solution.py:73
  32.6 0.1 reduce-scatter.3.cloned.1.call-start
  32.7 0.5 copy.55
  33.2 205.9 %all-to-all-done = f32[16,24,48,128]{3,2,1,0:T(8,128)} async-done(((f32[16,24,48,128]{3,2,1,0:T(8,128)}), f32[16,24,48,128]{3,2,1,0:T(8,128)}, u32[]{:S(2)}, u32[]{:S(2)}) %all-to-all-start) | async-done | bytes 9437216 | tf_op jit(solution)/shard_map/all_to_all | solution.py:73
  239.1 9.8 %copy.54 = f32[384,48,128]{0,1,2:T(8,128)} copy(f32[384,48,128]{2,1,0:T(8,128)} %bitcast.6) | data formatting | bytes 18874368 | tf_op jit(solution)/shard_map/reshape | solution.py:72
  248.9 9.9 %convolution_bitcast_fusion.1 = f32[24,384,128]{1,0,2:T(8,128)} fusion(f32[384,48,128]{0,1,2:T(8,128)} %copy.54, f32[24,48,128]{1,0,2:T(8,128)S(1)} %copy.55), kind=kOutput, calls=%fused_computation.1 | convolution fusion | flops 679477248 | bytes 14745600 | tf_op jit(solution)/shard_map/ikh,jkh->ijh/dot_general | solution.py:69
  258.7 6.1 %copy.56 = f32[24,384,128]{2,0,1:T(8,128)} copy(f32[24,384,128]{1,0,2:T(8,128)} %convolution_bitcast_fusion.1) | data formatting | bytes 9437184 | tf_op jit(solution)/shard_map/ikh,jkh->ijh/transpose | solution.py:69
  264.9 0.1 reduce-scatter.3.cloned.1.call-update
  265.0 0.2 all-gather.2.cloned.1.call-start
  265.2 0.3 copy-done.3
  265.6 0.4 copy-done
  266.0 0.0 copy-done.5
  266.0 0.8 fusion.7
  266.8 67.5 %reduce-scatter.3.cloned.1.call-done = f32[24,48,128]{2,0,1:T(8,128)} async-done(((f32[24,384,128]{2,0,1:T(8,128)}), f32[24,48,128]{2,0,1:T(8,128)}) %reduce-scatter.3.cloned.1.call-update) | async-done | bytes 589840 | tf_op jit(solution)/shard_map/reduce_scatter | solution.py:77
  334.4 1.3 reduce_sum.74
  335.6 0.1 copy.57
  335.7 0.1 copy.58
  335.8 1.5 multiply_reduce_fusion.2
  337.3 0.1 copy.59
  337.4 0.1 copy.60
  337.4 1.4 multiply_add_fusion.1
  338.9 0.7 fusion.63
  339.6 0.4 multiply_reduce_fusion.1
  340.1 2.1 fusion.30
  342.1 1.2 slice_multiply_fusion
  343.3 0.1 all-gather.2.cloned.1.call-update
  343.3 0.3 reduce-scatter.5.cloned.1.call-start
  343.6 0.5 copy.62
  344.2 59.0 %all-gather.2.cloned.1.call-done = f32[24,384,128]{2,1,0:T(8,128)} async-done(((f32[24,48,128]{2,1,0:T(8,128)}), f32[24,384,128]{2,1,0:T(8,128)}) %all-gather.2.cloned.1.call-update) | async-done | bytes 4718608 | tf_op jit(solution)/shard_map/all_gather | solution.py:84
  403.2 6.2 %copy.63 = f32[24,384,128]{1,0,2:T(8,128)} copy(f32[24,384,128]{2,1,0:T(8,128)} %all-gather.2.cloned.1.call-done) | data formatting | bytes 9437184 | tf_op jit(solution)/shard_map/all_gather | solution.py:84
  409.4 11.8 %convolution_bitcast_fusion = f32[384,48,128]{0,1,2:T(8,128)} fusion(f32[24,48,128]{1,0,2:T(8,128)S(1)} %copy.62, f32[24,384,128]{1,0,2:T(8,128)} %copy.63), kind=kOutput, calls=%fused_computation | convolution fusion | flops 679477248 | bytes 14745600 | tf_op jit(solution)/shard_map/kih,kjh->ijh/dot_general | solution.py:82
  421.2 9.8 %copy.64 = f32[384,48,128]{2,1,0:T(8,128)} copy(f32[384,48,128]{0,1,2:T(8,128)} %convolution_bitcast_fusion) | data formatting | bytes 18874368 | tf_op jit(solution)/shard_map/kih,kjh->ijh/transpose | solution.py:82
  431.0 0.1 reduce-scatter.5.cloned.1.call-update
  431.0 0.8 fusion.3
  431.9 73.9 %reduce-scatter.5.cloned.1.call-done = f32[24,48,128]{2,1,0:T(8,128)} async-done(((f32[384,48,128]{2,1,0:T(8,128)}), f32[24,48,128]{2,1,0:T(8,128)}) %reduce-scatter.5.cloned.1.call-update) | async-done | bytes 589840 | tf_op jit(solution)/shard_map/reduce_scatter | solution.py:88
  505.8 1.3 reduce_sum.78
  507.1 1.5 multiply_reduce_fusion
  508.6 2.7 fusion
  (18 shorter events, 0.1 us)
Async XLA Ops:
  19.1 220.0 %all-to-all-start = ((f32[16,24,48,128]{3,2,1,0:T(8,128)}), f32[16,24,48,128]{3,2,1,0:T(8,128)}, u32[]{:S(2)}, u32[]{:S(2)}) async-start(f32[16,24,48,128]{3,2,1,0:T(8,128)} %stack.2), calls=%async_computation | async-start | bytes 18874368 | tf_op jit(solution)/shard_map/all_to_all | solution.py:73
  32.6 301.7 %reduce-scatter.3.cloned.1.call-start = ((), (), s32[]{:S(2)}) async-start(), calls=%async_computation.3 | async-start | bytes 5308416 | tf_op jit(solution)/shard_map/reduce_scatter | solution.py:77
  264.9 0.7 copy-start.3
  264.9 0.7 copy-start.4
  264.9 1.1 copy-start
  264.9 1.1 copy-start.5
  264.9 74.0 %copy-start.2 = (f32[2,128,128]{2,1,0:T(8,128)S(1)}, f32[2,128,128]{2,1,0:T(8,128)}, u32[]{:S(2)}) copy-start(f32[2,128,128]{2,1,0:T(8,128)} %param.17) | copy-start | bytes 393220
  265.0 75.1 %copy-start.1 = (f32[2,128,512]{2,1,0:T(8,128)S(1)}, f32[2,128,512]{2,1,0:T(8,128)}, u32[]{:S(2)}) copy-start(f32[2,128,512]{2,1,0:T(8,128)} %param.13) | copy-start | bytes 1572868
  265.0 138.2 %all-gather.2.cloned.1.call-start = ((), (), s32[]{:S(2)}) async-start(), calls=%async_computation.4 | async-start | bytes 5308416 | tf_op jit(solution)/shard_map/all_gather | solution.py:84
  343.3 162.4 %reduce-scatter.5.cloned.1.call-start = ((), (), s32[]{:S(2)}) async-start(), calls=%async_computation.5 | async-start | bytes 10027008 | tf_op jit(solution)/shard_map/reduce_scatter | solution.py:88
Sparse Core Ops, SparseCore 0:
  265.1 69.2 reduce-scatter.2
  343.5 59.7 all-gather.1
  431.2 74.5 reduce-scatter.4
